TPU v7x, 512 devices: a whole 4x8x8 slice. The times are simulated.
512 devices in a mesh: row: 32 (over z_lo, y, core), col: 16 (over z_hi, x).
Axes of the slice: x: 4, y: 8, z: 8 (z_hi: 4, z_lo: 2; z = z_hi * 2 + z_lo), core: 2. Of those that a mesh axis runs over, the one named last changes fastest.
Arguments:
- pixels: float32 [8, 3, 1024, 2048], P(None, None, 'row', 'col'), may hold values from -6 to 6
- factor: float32 [1024, 512], P('row'), may hold values from -6 to 6
Outputs:
- gram: float32 [1024, 1024], P('row', 'col')
- projected: float32 [1024, 512], P('col', 'row')
All inputs are finite; a program needn't handle non-finite values.
Results may differ from a plain program's by a relative error of at most 0.000075.
Values sent between devices are 32-bit elements; how exact they have to be, the bound alone decides.
No kernel may reach another device: no remote copies, remote signals or barrier semaphores. Data moves between devices by JAX's collectives and lax.ppermute only.
A program may use at most 64 MiB of HBM per device.

v0:
```python
import jax
import jax.numpy as jnp
from jax import lax
from jax.sharding import PartitionSpec as P


def split_up(array, dim, size):
    before, after = (array.shape[:dim], array.shape[dim + 1 :])
    return jnp.moveaxis(array.reshape(*before, size, -1, *after), dim, 0)


def sum_at_owner(array, axis, dim):
    size = lax.axis_size(axis)
    parts = lax.all_to_all(split_up(array, dim, size), axis, 0, 0, tiled=True)
    return jnp.sum(parts, axis=0)


def pair_rows(own, others):
    return jnp.einsum(
        "vciw,vcjw->ij",
        own,
        others,
        precision=lax.Precision.HIGHEST,
        preferred_element_type=jnp.float32,
    )


def shards(pixels, factor):
    col_count = lax.axis_size("col")
    weight_scale = 1.0 / (pixels.shape[0] * pixels.shape[1] * pixels.shape[3] * col_count)
    partial_value = pair_rows(pixels, lax.all_gather(pixels, "row", axis=2, tiled=True))
    partial_value = partial_value * weight_scale
    block = sum_at_owner(partial_value, "col", 1)
    term = lax.dot_general(
        block,
        factor,
        (((0,), (0,)), ((), ())),
        precision=lax.Precision.HIGHEST,
        preferred_element_type=jnp.float32,
    )
    projected = sum_at_owner(term, "row", 1)
    return (block, projected)


def solution(mesh):
    in_specs = (P(None, None, "row", "col"), P("row", None))
    out_specs = (P("row", "col"), P("col", "row"))
    return jax.shard_map(shards, mesh=mesh, in_specs=in_specs, out_specs=out_specs, check_vma=False)
```

profile of v0, /device:TPU:1, one launch (start us, length us, event | category | flops | bytes accessed | tf_op | source)
XLA Modules:
  0.0 160.4 jit_solution(10644495970476327923)
XLA Ops:
  7.2 0.0 copy-start
  7.2 0.0 all-gather.2.cloned.1.call-start
  7.2 1.8 %copy.12 = f32[8,3,32,128]{3,2,0,1:T(8,128)} copy(f32[8,3,32,128]{3,2,1,0:T(8,128)} %param.2) | data formatting | bytes 786432 | tf_op args[0]
  9.0 0.0 all-gather.2.cloned.1.call-update
  9.0 89.4 %all-gather.2.cloned.1.call-done = f32[8,3,1024,128]{3,2,0,1:T(8,128)} async-done(((f32[8,3,32,128]{3,2,0,1:T(8,128)}), f32[8,3,1024,128]{3,2,0,1:T(8,128)}) %all-gather.2.cloned.1.call-update) | async-done | bytes 12582928 | tf_op jit(solution)/shard_map/all_gather | solution.py:31
  98.4 14.3 %fusion = f32[32,1024]{1,0:T(8,128)S(1)} fusion(f32[8,3,1024,128]{3,2,0,1:T(8,128)} %all-gather.2.cloned.1.call-done, f32[8,3,32,128]{3,2,1,0:T(8,128)} %param.2), kind=kOutput, calls=%fused_computation.2 | convolution fusion | flops 1207992320 | bytes 13107200 | tf_op jit(solution)/shard_map/vciw,vcjw->ij/dot_general | solution.py:19
  112.7 0.1 reshape.9
  112.8 0.1 copy.24
  112.9 0.8 reshape.12
  113.8 9.5 %all-to-all-start = ((f32[16,1,2048]{2,1,0:T(1,128)}), f32[16,1,2048]{2,1,0:T(1,128)S(1)}, u32[]{:S(2)}, u32[]{:S(2)}) async-start(f32[16,1,2048]{2,1,0:T(1,128)} %reshape.12), calls=%async_computation | async-start | bytes 262144 | tf_op jit(solution)/shard_map/all_to_all | solution.py:14
  123.3 0.0 copy-done
  123.3 0.1 copy.14
  123.4 9.2 %all-to-all-done = f32[16,1,2048]{2,1,0:T(1,128)S(1)} async-done(((f32[16,1,2048]{2,1,0:T(1,128)}), f32[16,1,2048]{2,1,0:T(1,128)S(1)}, u32[]{:S(2)}, u32[]{:S(2)}) %all-to-all-start) | async-done | bytes 131104 | tf_op jit(solution)/shard_map/all_to_all | solution.py:14
  132.6 0.5 broadcast
  133.1 0.9 reduce
  134.1 0.1 reshape.13
  134.2 0.0 copy-start.1
  134.2 0.4 convolution_bitcast_fusion
  134.6 0.2 copy.25
  134.8 0.2 reshape.14
  135.0 16.9 %all_to_all.10 = f32[32,1,1024]{2,1,0:T(1,128)S(1)} all-to-all(f32[32,1,1024]{2,1,0:T(1,128)S(1)} %reshape.14), channel_id=1, replica_groups=mesh['row'=32,'col'=16] {'row'}, dimensions={0} | all-to-all | bytes 262144 | tf_op jit(solution)/shard_map/all_to_all | solution.py:14
  151.9 1.0 reduce.1
  152.8 0.1 reshape.15
  152.9 0.6 bitcast_reduce_fusion
  153.6 0.0 copy-done.1
  (1 shorter events, 0.0 us)
Async XLA Ops:
  7.2 116.1 %copy-start = (f32[32,512]{1,0:T(8,128)S(1)}, f32[32,512]{1,0:T(8,128)}, u32[]{:S(2)}) copy-start(f32[32,512]{1,0:T(8,128)} %param.3) | copy-start | bytes 196612
  7.2 91.2 %all-gather.2.cloned.1.call-start = ((), (), s32[]{:S(2)}) async-start(), calls=%async_computation.2 | async-start | bytes 12976128 | tf_op jit(solution)/shard_map/all_gather | solution.py:31
  113.8 18.8 %all-to-all-start = ((f32[16,1,2048]{2,1,0:T(1,128)}), f32[16,1,2048]{2,1,0:T(1,128)S(1)}, u32[]{:S(2)}, u32[]{:S(2)}) async-start(f32[16,1,2048]{2,1,0:T(1,128)} %reshape.12), calls=%async_computation | async-start | bytes 262144 | tf_op jit(solution)/shard_map/all_to_all | solution.py:14
  134.2 19.4 %copy-start.1 = (f32[32,64]{1,0:T(8,128)}, f32[32,64]{1,0:T(8,128)S(1)}, u32[]{:S(2)}) copy-start(f32[32,64]{1,0:T(8,128)S(1)} %reduce_sum.18) | copy-start | bytes 24580
Sparse Core Ops, SparseCore 0:
  10.1 88.2 all-gather.1
where the time goes:
time: 161 us; the launch traced here: 160 us
  waiting for transfers between devices  98.6 us (61%)
  blocking collectives  16.9 us (10%)
  matrix products  14.7 us (9%)
  between operations  14.1 us (9%)
  starting transfers between devices  9.53 us (6%)
  local copies, waits for them, and re-layouts  3.99 us (2%)
  other arithmetic  2.57 us (2%)
    all_gather x1, waiting for transfers between devices, shards(): lax.all_gather(pixels, 'row', axis=2, tiled=True)  89.4 us
    all_to_all x1, blocking collectives, sum_at_owner(): parts = lax.all_to_all(split_up(array, dim, size), axis, 0, 0, tiled=True)  16.9 us
    dot_general x1, matrix products, pair_rows(): jnp.einsum('vciw,vcjw->ij', own, others, precision=lax.Precision.HIGHEST,...  14.3 us
    all_to_all x1, starting transfers between devices, sum_at_owner(): parts = lax.all_to_all(split_up(array, dim, size), axis, 0, 0, tiled=True)  9.49 us
    all_to_all x1, waiting for transfers between devices, sum_at_owner(): parts = lax.all_to_all(split_up(array, dim, size), axis, 0, 0, tiled=True)  9.19 us
  transfers between devices with their start and end apart: 2, of which 2 were waited for; matrix products, arithmetic and copies ran while one was open for 0% of the time, Pallas kernels for 0%

commit v1 on v0

--- a/solution.py
+++ b/solution.py
@@ -2,6 +2,13 @@
 import jax.numpy as jnp
 from jax import lax
 from jax.sharding import PartitionSpec as P
+
+
+def all_by_exchange(x, name, dim):
+    n_dev = lax.axis_size(name)
+    blocks = jnp.stack([x for _ in range(n_dev)])
+    blocks = lax.all_to_all(blocks, name, split_axis=0, concat_axis=0)
+    return jnp.concatenate(blocks, axis=dim)
 
 
 def split_up(array, dim, size):
@@ -28,7 +35,7 @@
 def shards(pixels, factor):
     col_count = lax.axis_size("col")
     weight_scale = 1.0 / (pixels.shape[0] * pixels.shape[1] * pixels.shape[3] * col_count)
-    partial_value = pair_rows(pixels, lax.all_gather(pixels, "row", axis=2, tiled=True))
+    partial_value = pair_rows(pixels, all_by_exchange(pixels, "row", 2))
     partial_value = partial_value * weight_scale
     block = sum_at_owner(partial_value, "col", 1)
     term = lax.dot_general(

time: 161 us -> 356 us (2.21)
  blocking collectives: 16.9 us -> 300 us
  waiting for transfers between devices: 98.6 us -> 9.22 us
  between operations: 14.1 us -> 0.74 us
  local copies, waits for them, and re-layouts: 3.99 us -> 16.2 us
    all_to_all x0 -> x1, blocking collectives: none -> 284 us  [all_by_exchange(): blocks = lax.all_to_all(blocks, name, split_axis=0, concat_axis=0)]
    all_gather x1 -> x0, waiting for transfers between devices: 89.4 us -> none  [shards(): lax.all_gather(pixels, 'row', axis=2, tiled=True)]
    reshape x0 -> x1, local copies, waits for them, and re-layouts: none -> 11.4 us  [all_by_exchange(): return jnp.concatenate(blocks, axis=dim)]
  transfers between devices with their start and end apart: 2 -> 1, of which waited for: 2 -> 1; matrix products, arithmetic and copies ran while one was open for 0% -> 0% of each run, Pallas kernels for 0% -> 0%
where the time goes in v1:
time: 356 us; the launch traced here: 355 us
  blocking collectives  300 us (84%)
  local copies, waits for them, and re-layouts  16.2 us (5%)
  matrix products  14.7 us (4%)
  starting transfers between devices  11.7 us (3%)
  waiting for transfers between devices  9.22 us (3%)
    all_to_all x1, blocking collectives, all_by_exchange(): blocks = lax.all_to_all(blocks, name, split_axis=0, concat_axis=0)  284 us
    all_to_all x1, blocking collectives, sum_at_owner(): parts = lax.all_to_all(split_up(array, dim, size), axis, 0, 0, tiled=True)  16.1 us
    dot_general x1, matrix products, pair_rows(): jnp.einsum('vciw,vcjw->ij', own, others, precision=lax.Precision.HIGHEST,...  14.3 us
    all_to_all x1, starting transfers between devices, sum_at_owner(): parts = lax.all_to_all(split_up(array, dim, size), axis, 0, 0, tiled=True)  11.7 us
    reshape x1, local copies, waits for them, and re-layouts, all_by_exchange(): return jnp.concatenate(blocks, axis=dim)  11.4 us
    all_to_all x1, waiting for transfers between devices, sum_at_owner(): parts = lax.all_to_all(split_up(array, dim, size), axis, 0, 0, tiled=True)  9.22 us
  transfers between devices with their start and end apart: 1, of which 1 were waited for; matrix products, arithmetic and copies ran while one was open for 0% of the time, Pallas kernels for 0%

profile of v1, /device:TPU:1, one launch (start us, length us, event | category | flops | bytes accessed | tf_op | source)
XLA Modules:
  0.0 355.4 jit_solution(3980428004158320097)
XLA Ops:
  0.6 1.0 copy.13
  1.7 1.6 stack.2
  3.3 284.2 %all_to_all.15 = f32[32,8,3,32,128]{4,3,1,2,0:T(8,128)} all-to-all(f32[32,8,3,32,128]{4,3,1,2,0:T(8,128)S(1)} %stack.2), channel_id=1, replica_groups=mesh['row'=32,'col'=16] {'row'}, dimensions={0} | all-to-all | bytes 25165824 | tf_op jit(solution)/shard_map/all_to_all | solution.py:10
  287.4 0.0 copy-start
  287.4 11.4 %copy.12 = f32[8,3,32,32,128]{4,3,2,0,1:T(8,128)} copy(f32[8,3,32,32,128]{4,3,0,1,2:T(8,128)} %bitcast.25) | data formatting | bytes 25165824 | tf_op jit(solution)/shard_map/reshape | solution.py:11
  298.8 0.0 copy-start.1
  298.8 0.0 copy-done
  298.8 14.3 %fusion = f32[32,1024]{1,0:T(8,128)S(1)} fusion(f32[8,3,1024,128]{3,2,0,1:T(8,128)} %bitcast.26, f32[8,3,32,128]{3,2,1,0:T(8,128)S(1)} %copy-done), kind=kOutput, calls=%fused_computation.2 | convolution fusion | flops 1207992320 | bytes 13107200 | tf_op jit(solution)/shard_map/vciw,vcjw->ij/dot_general | solution.py:26
  313.2 0.1 reshape.19
  313.3 0.1 copy.25
  313.4 0.8 reshape.22
  314.2 11.7 %all-to-all-start.1 = ((f32[16,1,2048]{2,1,0:T(1,128)}), f32[16,1,2048]{2,1,0:T(1,128)S(1)}, u32[]{:S(2)}, u32[]{:S(2)}) async-start(f32[16,1,2048]{2,1,0:T(1,128)} %reshape.22), calls=%async_computation.1 | async-start | bytes 262144 | tf_op jit(solution)/shard_map/all_to_all | solution.py:21
  325.9 0.0 copy-done.1
  325.9 0.1 copy.15
  326.0 9.2 %all-to-all-done.1 = f32[16,1,2048]{2,1,0:T(1,128)S(1)} async-done(((f32[16,1,2048]{2,1,0:T(1,128)}), f32[16,1,2048]{2,1,0:T(1,128)S(1)}, u32[]{:S(2)}, u32[]{:S(2)}) %all-to-all-start.1) | async-done | bytes 131104 | tf_op jit(solution)/shard_map/all_to_all | solution.py:21
  335.2 0.5 broadcast.2
  335.7 0.9 reduce
  336.7 0.1 reshape.23
  336.8 0.0 copy-start.2
  336.9 0.4 convolution_bitcast_fusion
  337.2 0.2 copy.26
  337.4 0.2 reshape.24
  337.6 16.1 %all_to_all.16 = f32[32,1,1024]{2,1,0:T(1,128)S(1)} all-to-all(f32[32,1,1024]{2,1,0:T(1,128)S(1)} %reshape.24), channel_id=1, replica_groups=mesh['row'=32,'col'=16] {'row'}, dimensions={0} | all-to-all | bytes 262144 | tf_op jit(solution)/shard_map/all_to_all | solution.py:21
  353.7 1.0 reduce.1
  354.7 0.1 reshape.25
  354.8 0.6 bitcast_reduce_fusion
  355.4 0.0 copy-done.2
  (1 shorter events, 0.0 us)
Async XLA Ops:
  287.4 11.4 %copy-start = (f32[8,3,32,128]{3,2,1,0:T(8,128)S(1)}, f32[8,3,32,128]{3,2,1,0:T(8,128)}, u32[]{:S(2)}) copy-start(f32[8,3,32,128]{3,2,1,0:T(8,128)} %param.2) | copy-start | bytes 1179652
  298.8 27.1 %copy-start.1 = (f32[32,512]{1,0:T(8,128)S(1)}, f32[32,512]{1,0:T(8,128)}, u32[]{:S(2)}) copy-start(f32[32,512]{1,0:T(8,128)} %param.3) | copy-start | bytes 196612
  314.2 21.1 %all-to-all-start.1 = ((f32[16,1,2048]{2,1,0:T(1,128)}), f32[16,1,2048]{2,1,0:T(1,128)S(1)}, u32[]{:S(2)}, u32[]{:S(2)}) async-start(f32[16,1,2048]{2,1,0:T(1,128)} %reshape.22), calls=%async_computation.1 | async-start | bytes 262144 | tf_op jit(solution)/shard_map/all_to_all | solution.py:21
  336.8 18.6 %copy-start.2 = (f32[32,64]{1,0:T(8,128)}, f32[32,64]{1,0:T(8,128)S(1)}, u32[]{:S(2)}) copy-start(f32[32,64]{1,0:T(8,128)S(1)} %reduce_sum.18) | copy-start | bytes 24580
